TPU v7x, 32 devices: a 4x4x1 block of a 4x4x8 slice. The times are simulated.
32 devices in a mesh: spin: 1 (over z), row: 4 (over y), col: 8 (over x, core).
Axes of the slice: x: 4, y: 4, z: 1, core: 2. Of those that a mesh axis runs over, the one named last changes fastest.
The devices are a block of a 4x4x8 slice.
Arguments:
- hamiltonian: float32 [3072, 3072], P(('spin', 'row'), 'col')
- bounds: float32 [2], P('spin')
- n_occ: int32 [1], P('spin')
Outputs:
- output 1: float32 [3072, 3072], P(('spin', 'row'), 'col')
- output 2: float32 [1], P('spin')
All inputs are finite; a program needn't handle non-finite values.
Results may differ from a plain program's by a relative error of at most 0.001.
Values sent between devices are 32-bit elements.
A program may use at most 768 MiB of HBM per device.

v0:
```python
import jax
import jax.numpy as jnp
from jax import lax
from jax.sharding import PartitionSpec as P

STEPS = 3


def solution(mesh):
    n_cols = mesh.shape["col"]
    highest = lax.Precision.HIGHEST

    def local_fn(ham_blk, bounds, n_occ):
        rows_n, cols_n = ham_blk.shape
        mat_order = cols_n * n_cols
        row_ids = lax.axis_index("row") * rows_n + lax.broadcasted_iota(jnp.int32, (rows_n, 1), 0)
        col_ids = lax.axis_index("col") * cols_n + lax.broadcasted_iota(jnp.int32, (1, cols_n), 1)
        diag_mask = row_ids == col_ids
        occupied = n_occ[0].astype(jnp.float32)
        mu_val = lax.psum(jnp.sum(jnp.where(diag_mask, ham_blk, 0.0)), ("row", "col")) / mat_order
        lam_scale = jnp.minimum(occupied / (bounds[1] - mu_val), (mat_order - occupied) / (mu_val - bounds[0]))
        density = jnp.where(diag_mask, (lam_scale * mu_val + occupied) / mat_order, 0.0) - (lam_scale / mat_order) * ham_blk
        for _ in range(STEPS):
            x_rows = lax.all_gather(density, "col", axis=1, tiled=True)
            x_cols = lax.all_gather(density, "row", axis=0, tiled=True)
            dens_sq = jnp.dot(x_rows, x_cols, precision=highest, preferred_element_type=jnp.float32)
            sq_rows = lax.all_gather(dens_sq, "col", axis=1, tiled=True)
            dens_cube = jnp.dot(sq_rows, x_cols, precision=highest, preferred_element_type=jnp.float32)
            part_sums = jnp.stack([jnp.sum(jnp.where(diag_mask, density, 0.0)), jnp.sum(density * density), jnp.sum(dens_sq * density)])
            traces = lax.psum(part_sums, ("row", "col"))
            mix_coef = (traces[1] - traces[2]) / (traces[0] - traces[1])
            density = ((1.0 - 2.0 * mix_coef) * density + (1.0 + mix_coef) * dens_sq - dens_cube) / (1.0 - mix_coef)
        energy = 2.0 * lax.psum(jnp.sum(density * ham_blk), ("row", "col"))
        return density, energy[None]

    spec_mat = P(("spin", "row"), "col")
    return jax.shard_map(local_fn, mesh=mesh, in_specs=(spec_mat, P("spin"), P("spin")), out_specs=(spec_mat, P("spin")), check_vma=False)
```

profile of v0, /device:TPU:97, one launch (start us, length us, event | category | flops | bytes accessed | tf_op | source)
XLA Modules:
  0.0 703.2 jit_solution(12698834693693705805)
XLA Ops:
  7.3 2.2 fusion.3
  9.6 49.7 %psum.35 = f32[]{:T(128)} all-reduce(f32[]{:T(128)} %fusion.3), channel_id=1, replica_groups=mesh['spin'=1,'row'=4,'col'=8] {'row','col'}, use_global_device_ids=true, to_apply=%region_1.2 | all-reduce | flops 1 | bytes 8 | tf_op jit(solution)/shard_map/psum | solution.py:20
  64.7 47.1 %all-gather.12.cloned.1.call-done = f32[3072,384]{1,0:T(8,128)} async-done(((f32[768,384]{1,0:T(8,128)}), f32[3072,384]{1,0:T(8,128)}) %all-gather.12.cloned.1.call-update) | async-done | bytes 4718608 | tf_op jit(solution)/shard_map/all_gather | solution.py:25
  111.8 54.7 %all-gather.10.cloned.1.call-done = f32[768,3072]{1,0:T(8,128)} async-done(((f32[768,384]{1,0:T(8,128)}), f32[768,3072]{1,0:T(8,128)}) %all-gather.10.cloned.1.call-update) | async-done | bytes 9437200 | tf_op jit(solution)/shard_map/all_gather | solution.py:24
  166.5 19.5 %fusion.5 = (f32[]{:T(128)}, f32[]{:T(128)}, f32[]{:T(128)}, f32[768,384]{1,0:T(8,128)}) fusion(f32[768,384]{1,0:T(8,128)S(1)} %copy-done.2, s32[384]{0:T(512)S(1)} %iota_add_fusion.1, s32[768]{0:T(1024)S(1)} %iota_add_fusion, f32[768,3072]{1,0:T(8,128)} %all-gather.10.cloned.1.call-done, f32[3072,384]{1,0:T(8,128)} %all-gather.12.cloned.1.call-done), kind=kOutput, calls=%fused_computation.13 | convolution fusion | flops 10873700352 | bytes 16519692 | tf_op jit(solution)/shard_map/dot_general | solution.py:26
  186.1 2.0 pad_maximum_fusion
  188.1 46.6 %psum.36 = f32[3]{0:T(128)S(1)} all-reduce(f32[3]{0:T(128)S(1)} %pad_maximum_fusion), channel_id=1, replica_groups=mesh['spin'=1,'row'=4,'col'=8] {'row','col'}, use_global_device_ids=true, to_apply=%region_5.6 | all-reduce | flops 3 | bytes 24 | tf_op jit(solution)/shard_map/psum | solution.py:30
  237.9 1.5 all-gather.14.cloned.1.call-done
  239.3 18.7 %fusion = f32[768,384]{1,0:T(8,128)} fusion(f32[768,3072]{1,0:T(8,128)} %all-gather.14.cloned.1.call-done, f32[3072,384]{1,0:T(8,128)} %all-gather.12.cloned.1.call-done, f32[768,384]{1,0:T(8,128)S(1)} %copy-done.4, f32[768,384]{1,0:T(8,128)S(1)} %copy-done.2, f32[]{:T(128)} %bitcast.8, f32[]{:T(128)} %bitcast.7, f32[]{:T(128)} %bitcast.6), kind=kOutput, calls=%fused_computation.8 | convolution fusion | flops 10873110528 | bytes 17694732 | tf_op jit(solution)/shard_map/dot_general | solution.py:28
  259.1 48.2 %all-gather.18.cloned.1.call-done = f32[3072,384]{1,0:T(8,128)} async-done(((f32[768,384]{1,0:T(8,128)}), f32[3072,384]{1,0:T(8,128)}) %all-gather.18.cloned.1.call-update) | async-done | bytes 4718608 | tf_op jit(solution)/shard_map/all_gather | solution.py:25
  307.2 54.5 %all-gather.16.cloned.1.call-done = f32[768,3072]{1,0:T(8,128)} async-done(((f32[768,384]{1,0:T(8,128)}), f32[768,3072]{1,0:T(8,128)}) %all-gather.16.cloned.1.call-update) | async-done | bytes 9437200 | tf_op jit(solution)/shard_map/all_gather | solution.py:24
  361.8 19.5 %fusion.6 = (f32[]{:T(128)}, f32[]{:T(128)}, f32[]{:T(128)}, f32[768,384]{1,0:T(8,128)}) fusion(f32[768,384]{1,0:T(8,128)S(1)} %copy-done.1, s32[384]{0:T(512)S(1)} %iota_add_fusion.1, s32[768]{0:T(1024)S(1)} %iota_add_fusion, f32[768,3072]{1,0:T(8,128)} %all-gather.16.cloned.1.call-done, f32[3072,384]{1,0:T(8,128)} %all-gather.18.cloned.1.call-done), kind=kOutput, calls=%fused_computation.14 | convolution fusion | flops 10873700352 | bytes 16519692 | tf_op jit(solution)/shard_map/dot_general | solution.py:26
  381.4 2.0 pad_maximum_fusion.1
  383.4 46.6 %psum.37 = f32[3]{0:T(128)S(1)} all-reduce(f32[3]{0:T(128)S(1)} %pad_maximum_fusion.1), channel_id=1, replica_groups=mesh['spin'=1,'row'=4,'col'=8] {'row','col'}, use_global_device_ids=true, to_apply=%region_9.10 | all-reduce | flops 3 | bytes 24 | tf_op jit(solution)/shard_map/psum | solution.py:30
  433.2 1.5 all-gather.20.cloned.1.call-done
  434.6 18.7 %fusion.1 = f32[768,384]{1,0:T(8,128)} fusion(f32[768,3072]{1,0:T(8,128)} %all-gather.20.cloned.1.call-done, f32[3072,384]{1,0:T(8,128)} %all-gather.18.cloned.1.call-done, f32[768,384]{1,0:T(8,128)S(1)} %copy-done.5, f32[768,384]{1,0:T(8,128)S(1)} %copy-done.1, f32[]{:T(128)} %bitcast.14, f32[]{:T(128)} %bitcast.13, f32[]{:T(128)} %bitcast.12), kind=kOutput, calls=%fused_computation.9 | convolution fusion | flops 10873110528 | bytes 17694732 | tf_op jit(solution)/shard_map/dot_general | solution.py:28
  454.6 48.0 %all-gather.24.cloned.1.call-done = f32[3072,384]{1,0:T(8,128)} async-done(((f32[768,384]{1,0:T(8,128)}), f32[3072,384]{1,0:T(8,128)}) %all-gather.24.cloned.1.call-update) | async-done | bytes 4718608 | tf_op jit(solution)/shard_map/all_gather | solution.py:25
  502.5 54.7 %all-gather.22.cloned.1.call-done = f32[768,3072]{1,0:T(8,128)} async-done(((f32[768,384]{1,0:T(8,128)}), f32[768,3072]{1,0:T(8,128)}) %all-gather.22.cloned.1.call-update) | async-done | bytes 9437200 | tf_op jit(solution)/shard_map/all_gather | solution.py:24
  557.2 19.5 %fusion.7 = (f32[]{:T(128)}, f32[]{:T(128)}, f32[]{:T(128)}, f32[768,384]{1,0:T(8,128)}) fusion(f32[768,384]{1,0:T(8,128)S(1)} %copy-done, s32[384]{0:T(512)S(1)} %iota_add_fusion.1, s32[768]{0:T(1024)S(1)} %iota_add_fusion, f32[768,3072]{1,0:T(8,128)} %all-gather.22.cloned.1.call-done, f32[3072,384]{1,0:T(8,128)} %all-gather.24.cloned.1.call-done), kind=kOutput, calls=%fused_computation.15 | convolution fusion | flops 10873700352 | bytes 16519692 | tf_op jit(solution)/shard_map/dot_general | solution.py:26
  576.7 2.1 pad_maximum_fusion.2
  578.8 46.6 %psum.38 = f32[3]{0:T(128)S(1)} all-reduce(f32[3]{0:T(128)S(1)} %pad_maximum_fusion.2), channel_id=1, replica_groups=mesh['spin'=1,'row'=4,'col'=8] {'row','col'}, use_global_device_ids=true, to_apply=%region_13.14 | all-reduce | flops 3 | bytes 24 | tf_op jit(solution)/shard_map/psum | solution.py:30
  628.6 1.5 all-gather.26.cloned.1.call-done
  630.1 20.2 %multiply_reduce_fusion = (f32[]{:T(128)}, f32[768,384]{1,0:T(8,128)}) fusion(f32[768,384]{1,0:T(8,128)S(1)} %copy-done.6, f32[]{:T(128)} %bitcast.20, f32[768,3072]{1,0:T(8,128)} %all-gather.26.cloned.1.call-done, f32[3072,384]{1,0:T(8,128)} %all-gather.24.cloned.1.call-done, f32[768,384]{1,0:T(8,128)S(1)} %copy-done.3, f32[]{:T(128)} %bitcast.19, ...), kind=kOutput, calls=%fused_computation.16 | convolution fusion | flops 10873700352 | bytes 18874384 | tf_op jit(solution)/shard_map/dot_general | solution.py:28
  650.3 44.6 %psum.39 = f32[]{:T(128)} all-reduce(f32[]{:T(128)} %get-tuple-element.25), channel_id=1, replica_groups=mesh['spin'=1,'row'=4,'col'=8] {'row','col'}, use_global_device_ids=true, to_apply=%region_15.16 | all-reduce | flops 1 | bytes 8 | tf_op jit(solution)/shard_map/psum | solution.py:33
  (41 shorter events, 7.2 us)
Async XLA Ops:
  7.2 55.4 %copy-start.6 = (f32[768,384]{1,0:T(8,128)S(1)}, f32[768,384]{1,0:T(8,128)}, u32[]{:S(2)}) copy-start(f32[768,384]{1,0:T(8,128)} %param.3) | copy-start | bytes 3538948
  7.2 52.1 %copy-start.7 = (f32[2]{0:T(128)S(1)}, f32[2]{0:T(128)}, u32[]{:S(2)}) copy-start(f32[2]{0:T(128)} %param.4) | copy-start | bytes 28
  7.2 104.6 %all-gather.12.cloned.1.call-start = ((), (), s32[]{:S(2)}) async-start(), calls=%async_computation.1 | async-start | bytes 5898240 | tf_op jit(solution)/shard_map/all_gather | solution.py:25
  63.8 102.7 %copy-start.2 = (f32[768,384]{1,0:T(8,128)S(1)}, f32[768,384]{1,0:T(8,128)}, u32[]{:S(2)}) copy-start(f32[768,384]{1,0:T(8,128)} %fusion.4) | copy-start | bytes 3538948
  63.8 102.6 %all-gather.10.cloned.1.call-start = ((), (), s32[]{:S(2)}) async-start(), calls=%async_computation | async-start | bytes 10616832 | tf_op jit(solution)/shard_map/all_gather | solution.py:24
  64.7 174.7 %all-gather.14.cloned.1.call-start = ((), (), s32[]{:S(2)}) async-start(), calls=%async_computation.2 | async-start | bytes 10616832 | tf_op jit(solution)/shard_map/all_gather | solution.py:27
  185.9 53.4 %copy-start.4 = (f32[768,384]{1,0:T(8,128)S(1)}, f32[768,384]{1,0:T(8,128)}, u32[]{:S(2)}) copy-start(f32[768,384]{1,0:T(8,128)} %get-tuple-element.22) | copy-start | bytes 3538948
  186.0 121.2 %all-gather.18.cloned.1.call-start = ((), (), s32[]{:S(2)}) async-start(), calls=%async_computation.4 | async-start | bytes 5898240 | tf_op jit(solution)/shard_map/all_gather | solution.py:25
  258.1 103.7 %copy-start.1 = (f32[768,384]{1,0:T(8,128)S(1)}, f32[768,384]{1,0:T(8,128)}, u32[]{:S(2)}) copy-start(f32[768,384]{1,0:T(8,128)} %fusion) | copy-start | bytes 3538948
  258.2 103.6 %all-gather.16.cloned.1.call-start = ((), (), s32[]{:S(2)}) async-start(), calls=%async_computation.3 | async-start | bytes 10616832 | tf_op jit(solution)/shard_map/all_gather | solution.py:24
  258.8 175.8 %all-gather.20.cloned.1.call-start = ((), (), s32[]{:S(2)}) async-start(), calls=%async_computation.5 | async-start | bytes 10616832 | tf_op jit(solution)/shard_map/all_gather | solution.py:27
  381.2 53.4 %copy-start.5 = (f32[768,384]{1,0:T(8,128)S(1)}, f32[768,384]{1,0:T(8,128)}, u32[]{:S(2)}) copy-start(f32[768,384]{1,0:T(8,128)} %get-tuple-element.23) | copy-start | bytes 3538948
  381.3 121.3 %all-gather.24.cloned.1.call-start = ((), (), s32[]{:S(2)}) async-start(), calls=%async_computation.7 | async-start | bytes 5898240 | tf_op jit(solution)/shard_map/all_gather | solution.py:25
  453.4 103.8 %copy-start = (f32[768,384]{1,0:T(8,128)S(1)}, f32[768,384]{1,0:T(8,128)}, u32[]{:S(2)}) copy-start(f32[768,384]{1,0:T(8,128)} %fusion.1) | copy-start | bytes 3538948
  453.5 103.8 %all-gather.22.cloned.1.call-start = ((), (), s32[]{:S(2)}) async-start(), calls=%async_computation.6 | async-start | bytes 10616832 | tf_op jit(solution)/shard_map/all_gather | solution.py:24
  454.3 175.8 %all-gather.26.cloned.1.call-start = ((), (), s32[]{:S(2)}) async-start(), calls=%async_computation.8 | async-start | bytes 10616832 | tf_op jit(solution)/shard_map/all_gather | solution.py:27
  576.7 53.4 %copy-start.3 = (f32[768,384]{1,0:T(8,128)S(1)}, f32[768,384]{1,0:T(8,128)}, u32[]{:S(2)}) copy-start(f32[768,384]{1,0:T(8,128)} %get-tuple-element.24) | copy-start | bytes 3538948
Sparse Core Ops, SparseCore 0:
  64.0 47.7 all-gather.11
  114.0 52.4 all-gather.9
  186.1 53.1 all-gather.13
  258.3 48.9 all-gather.17
  309.2 52.4 all-gather.15
  381.4 53.1 all-gather.19
  453.6 48.9 all-gather.23
  504.7 52.4 all-gather.21
  576.9 53.1 all-gather.25
where the time goes:
time: 704 us; the launch traced here: 703 us
  waiting for transfers between devices  314 us (45%)
  blocking collectives  234 us (33%)
  matrix products  116 us (16%)
  between operations  26 us (4%)
  other arithmetic  9.61 us (1%)
    all_gather x3, waiting for transfers between devices, local_fn(): x_rows = lax.all_gather(density, 'col', axis=1, tiled=True)  164 us
    all_gather x3, waiting for transfers between devices, local_fn(): x_cols = lax.all_gather(density, 'row', axis=0, tiled=True)  143 us
    psum x3, blocking collectives, local_fn(): traces = lax.psum(part_sums, ('row', 'col'))  140 us
    dot_general x3, matrix products, local_fn(): jnp.dot(x_rows, x_cols, precision=highest, preferred_element_type=jnp.flo...  58.4 us
    dot_general x3, matrix products, local_fn(): jnp.dot(sq_rows, x_cols, precision=highest, preferred_element_type=jnp.fl...  57.7 us
    psum x1, blocking collectives, local_fn(): lax.psum(jnp.sum(jnp.where(diag_mask, ham_blk, 0.0)), ('row', 'col'))  49.7 us
    psum x1, blocking collectives, local_fn(): energy = 2.0 * lax.psum(jnp.sum(density * ham_blk), ('row', 'col'))  44.6 us
  transfers between devices with their start and end apart: 9, of which 9 were waited for; matrix products, arithmetic and copies ran while one was open for 1% of the time, Pallas kernels for 0%

commit v1 on v0

v1 whole, which is shorter than its diff:
```python
import functools

import jax
import jax.numpy as jnp
from jax import lax
from jax.experimental import pallas as pl
from jax.experimental.pallas import tpu as pltpu
from jax.sharding import PartitionSpec as P

STEPS = 3
RING = 4
CORES = 2
PARTS = 3
PIECES = 12
MESH = pl.DeviceIdType.MESH
HIGHEST = lax.Precision.HIGHEST


def purify(
    ham, bounds, n_occ, out, energy,
    cols, rows, sq, acc, tin, ham_t, red_a, red_b,
    x_recv, xf_recv, y_recv, yf_recv, d_recv, x_send, xf_send, y_send, yf_send, d_send,
    x2_recv, d2_recv, t_recv, x2_send, d2_send, t_send, a_recv, a_send, b_recv, b_send,
):
    cb, rb = ham.shape
    qr = rb // PARTS
    hr = qr // 2
    pr = rb // PIECES
    order = cb * RING
    per = PIECES // PARTS
    i = lax.axis_index("row")
    jc = lax.axis_index("col")
    j = lax.div(jc, CORES)
    c = lax.rem(jc, CORES)
    n_col = RING * CORES

    def wrap(v):
        return lax.rem(v + RING, RING)

    p = wrap(j - i)
    diag_chip = p == 0
    left, right = wrap(j + 3), wrap(j + 1)
    up, down = wrap(i + 3), wrap(i + 1)
    opp, iopp = wrap(j + 2), wrap(i + 2)
    partner = {"col": j * CORES + (1 - c)}
    to_x = ({"col": right * CORES + c}, {"col": left * CORES + c})
    to_y = ({"row": down}, {"row": up})
    half_cols = pl.ds(pl.multiple_of(c * rb, rb), rb)

    def copy(src, dst, send, recv, dev):
        return pltpu.make_async_remote_copy(
            src_ref=src, dst_ref=dst, send_sem=send, recv_sem=recv, device_id=dev, device_id_type=MESH
        )

    def send(ref, ss, rs, dev):
        copy(ref, ref, ss, rs, dev).start()

    def wait_recv(ref, rs):
        copy(ref, ref, d_send.at[0], rs, partner).wait_recv()

    def wait_send(ref, ss):
        copy(ref, ref, ss, d_recv.at[0, 0], partner).wait_send()

    def red_put(idx, vals):
        sub = lax.broadcasted_iota(jnp.int32, (8, 128), 0)
        tile = jnp.zeros((8, 128), jnp.float32)
        for r, v in enumerate(vals):
            tile = jnp.where(sub == r, v, tile)
        red_a[idx, jc] = tile

    def red_send(idx):
        for k in range(1, n_col):
            dev = lax.rem(jc + k, n_col)
            send(red_a.at[idx, jc], a_send.at[idx], a_recv.at[idx], {"col": dev})

    def red_mid_put(idx):
        wait_recv(red_a.at[idx, pl.ds(0, n_col - 1)], a_recv.at[idx])
        red_b[idx, i] = jnp.sum(red_a[idx], axis=0)

    def red_mid_send(idx):
        for k in range(1, RING):
            send(red_b.at[idx, i], b_send.at[idx], b_recv.at[idx], {"row": wrap(i + k)})

    def red_get(idx):
        wait_recv(red_b.at[idx, pl.ds(0, RING - 1)], b_recv.at[idx])
        wait_send(red_a.at[idx, pl.ds(0, n_col - 1)], a_send.at[idx])
        wait_send(red_b.at[idx, pl.ds(0, RING - 1)], b_send.at[idx])
        total = jnp.sum(red_b[idx], axis=0)
        return [total[r : r + 1, 0:1] for r in range(3)]

    def total_of(v):
        return jnp.sum(v, axis=1, keepdims=True)

    def is_diag(m):
        row_id = lax.broadcasted_iota(jnp.int32, (pr, cb), 0) + (m * pr + c * rb + (j - i) * cb)
        return row_id == lax.broadcasted_iota(jnp.int32, (pr, cb), 1)

    def piece_rows(m):
        return pl.ds(pl.multiple_of(lax.rem(m, per) * pr, pr), pr)

    def put_x(m, val, buf):
        cols[j, lax.div(m, per), c, piece_rows(m)] = val
        for q in range(PARTS):
            for h in range(CORES):
                at = h * rb + q * qr
                rows[buf, i, q, h, pl.ds(pl.multiple_of(m * pr, pr), pr)] = val[:, at : at + qr]

    barrier = pltpu.get_barrier_semaphore()
    for k in range(1, n_col):
        pl.semaphore_signal(barrier, inc=1, device_id={"col": lax.rem(jc + k, n_col)}, device_id_type=MESH)
    for k in range(1, RING):
        pl.semaphore_signal(barrier, inc=1, device_id={"row": wrap(i + k)}, device_id_type=MESH)
    for t in range(cb // qr):
        ham_t[:, t * qr : (t + 1) * qr] = ham[t * qr : (t + 1) * qr, :].T

    def trace_body(m, tr):
        blk = ham_t[pl.ds(pl.multiple_of(m * pr, pr), pr)]
        return tr + jnp.sum(jnp.where(is_diag(m), blk, 0.0), axis=0, keepdims=True)

    tr = lax.fori_loop(0, PIECES, trace_body, jnp.zeros((1, cb), jnp.float32))
    red_put(0, [total_of(tr)])
    pl.semaphore_wait(barrier, n_col + RING - 2)
    red_send(0)
    red_mid_put(0)
    red_mid_send(0)
    mu = red_get(0)[0] / order
    occ = jnp.full((1, 1), n_occ[0].astype(jnp.float32))
    eps_min = jnp.full((1, 1), bounds[0])
    eps_max = jnp.full((1, 1), bounds[1])
    lam = jnp.minimum(occ / (eps_max - mu), (order - occ) / (mu - eps_min)) / order

    @pl.loop(0, PIECES)
    def _(m):
        blk = ham_t[pl.ds(pl.multiple_of(m * pr, pr), pr)]
        put_x(m, jnp.where(is_diag(m), lam * (mu - blk) + occ / order, -lam * blk), 0)

    def step(s, carry):
        buf = lax.rem(s, 2)

        for q in range(PARTS):
            for o in range(2):
                for d in range(2):
                    h = d if o == 0 else 1 - d
                    send(cols.at[j, q, c, pl.ds(h * hr, hr)], x_send.at[d], x_recv.at[d, q, h], to_x[d])
                    send(rows.at[buf, i, q, h], y_send.at[d], y_recv.at[d, q, h], to_y[d])
            send(cols.at[j, q, c], d_send.at[0], d_recv.at[0, q], partner)
        acc[...] = jnp.zeros_like(acc)

        near = ((left, up), (right, down))

        def arrive_near(q):
            for d in range(2):
                kx, ky = near[d]
                xp = cols.at[kx, q, c, pl.ds(d * hr, hr)]
                wait_recv(xp, x_recv.at[d, q, d])
                send(xp, xf_send.at[d], xf_recv.at[d, q], to_x[d])
                yp = rows.at[buf, ky, q, d]
                wait_recv(yp, y_recv.at[d, q, d])
                send(yp, yf_send.at[d], yf_recv.at[d, q], to_y[d])
            for d in range(2):
                kx, ky = near[d]
                wait_recv(cols.at[kx, q, c, pl.ds((1 - d) * hr, hr)], x_recv.at[d, q, 1 - d])
                send(cols.at[kx, q, c], d_send.at[0], d_recv.at[3 if d == 0 else 1, q], partner)
                wait_recv(rows.at[buf, ky, q, 1 - d], y_recv.at[d, q, 1 - d])

        def arrive_far(q):
            for d in range(2):
                wait_recv(cols.at[opp, q, c, pl.ds(d * hr, hr)], xf_recv.at[d, q])
            send(cols.at[opp, q, c], d_send.at[0], d_recv.at[2, q], partner)
            for d in range(2):
                wait_recv(rows.at[buf, iopp, q, d], yf_recv.at[d, q])

        def item1(t, carry):
            in1 = t < jnp.where(diag_chip, 9, 6)
            late = jnp.maximum(t - 6, 0)
            q = jnp.where(
                in1,
                jnp.where(diag_chip, lax.div(t, 3), lax.div(t, 2)),
                jnp.where(diag_chip, jnp.maximum(t - 9, 0), lax.div(late, 2)),
            )
            u = jnp.where(
                in1,
                jnp.where(diag_chip, lax.rem(t, 3), lax.rem(t, 2)),
                jnp.where(diag_chip, 0, lax.rem(late, 2)),
            )
            k1 = jnp.where(
                diag_chip,
                i + jnp.where(u == 2, 3, u),
                jnp.where(p == 2, i + jnp.where(u == 0, 1, 3), jnp.where(u == 0, j, i)),
            )
            k = wrap(jnp.where(in1, k1, jnp.where(u == 0, i + 2, j + 2)))

            @pl.when(jnp.logical_and(in1, u == 0))
            def _():
                arrive_near(q)

            @pl.when(jnp.logical_and(jnp.logical_not(in1), u == 0))
            def _():
                arrive_far(q)

            wait_recv(cols.at[k, q, 1 - c], d_recv.at[wrap(k - j), q])
            rhs = cols[k, q].reshape(CORES * qr, cb)
            own = cols[k, q, :, :, half_cols].reshape(CORES * qr, rb)
            lhs = jnp.concatenate(
                [jnp.concatenate([rows[buf, k, q, h] for h in range(CORES)], axis=1), own.T], axis=0
            )
            acc[...] += jnp.dot(lhs, rhs, precision=HIGHEST, preferred_element_type=jnp.float32)
            return carry

        lax.fori_loop(0, RING * PARTS, item1, 0)
        for d in range(2):
            wait_send(cols.at[j, :, c], x_send.at[d])
            wait_send(cols.at[j, :, c, pl.ds(0, hr)], xf_send.at[d])
            wait_send(rows.at[buf, i], y_send.at[d])
            wait_send(rows.at[buf, i, :, 0], yf_send.at[d])
        wait_send(cols.at[:, :, c], d_send.at[0])

        for q in range(PARTS):
            sq[j, q, c] = acc[q * qr : (q + 1) * qr]

        @pl.when(jnp.logical_not(diag_chip))
        def _():
            for q in range(PARTS):
                sq[i, q, c] = acc[rb + q * qr : rb + (q + 1) * qr]

        def sums_body(m, carry):
            x = cols[j, lax.div(m, per), c, piece_rows(m)]
            x2 = acc[pl.ds(pl.multiple_of(m * pr, pr), pr)]
            t1 = jnp.sum(jnp.where(is_diag(m), x, 0.0), axis=0, keepdims=True)
            t2 = jnp.sum(x * x, axis=0, keepdims=True)
            t3 = jnp.sum(x2 * x, axis=0, keepdims=True)
            return carry[0] + t1, carry[1] + t2, carry[2] + t3

        zero = jnp.zeros((1, cb), jnp.float32)
        sums = lax.fori_loop(0, PIECES, sums_body, (zero, zero, zero))
        red_put(s + 1, [total_of(v) for v in sums])

        k_left = jnp.where(p == 1, opp, left)
        k_right = jnp.where(p == 3, opp, right)

        @pl.when(jnp.logical_not(diag_chip))
        def _():
            for m in range(PIECES):
                for d in range(2):
                    ref = sq.at[j, m // per, c, pl.ds((m % per) * pr, pr)]
                    send(ref, x2_send.at[d], x2_recv.at[d, m], to_x[d])

        @pl.when(p == 2)
        def _():
            for q in range(PARTS):
                for h in range(CORES):
                    src = sq.at[j, :, c, :, pl.ds(h * rb + q * qr, qr)]
                    copy(src, tin.at[q, h], t_send.at[0], t_recv.at[q, h], {"row": j}).start()

        for q in range(PARTS):
            send(sq.at[j, q, c], d2_send.at[0], d2_recv.at[0, q], partner)

        @pl.when(jnp.logical_not(diag_chip))
        def _():
            for q in range(PARTS):
                send(sq.at[i, q, c], d2_send.at[0], d2_recv.at[3, q], partner)

        red_send(s + 1)
        acc[0:rb] = jnp.zeros((rb, cb), jnp.float32)

        def arrive2(m):
            q = lax.div(m, per)
            u = lax.rem(m, per)
            for d, k in ((0, k_left), (1, k_right)):
                ref = sq.at[k, q, c, piece_rows(m)]
                wait_recv(ref, x2_recv.at[d, m])

                @pl.when(diag_chip)
                def _():
                    send(ref, x2_send.at[d], x2_recv.at[d, m], to_x[d])

            @pl.when(u == per - 1)
            def _():
                send(sq.at[k_left, q, c], d2_send.at[0], d2_recv.at[1, q], partner)
                send(sq.at[k_right, q, c], d2_send.at[0], d2_recv.at[2, q], partner)

            @pl.when(jnp.logical_and(diag_chip, u == per - 2))
            def _():
                for h in range(CORES):
                    wait_recv(tin.at[q, h], t_recv.at[q, h])
                    sq[opp, q, h, :, half_cols] = tin[q, h].reshape(rb, qr).T

            @pl.when(jnp.logical_and(diag_chip, u == per - 1))
            def _():
                ref = sq.at[opp, q, :, :, half_cols]
                send(ref, d2_send.at[0], d2_recv.at[3, q], partner)

        def item2(m, carry):
            @pl.when(m < PIECES)
            def _():
                arrive2(m)

            @pl.when(m == 3)
            def _():
                red_mid_put(s + 1)

            @pl.when(m == 4)
            def _():
                red_mid_send(s + 1)

            u = lax.rem(m, 4)
            qq = jnp.maximum(lax.div(m, 4) - 1, 0)
            early = m < 4
            kind = jnp.where(early, jnp.where(m < 3, 0, 3), u + 1)
            q = jnp.where(
                early, jnp.where(m < 3, m, 0), jnp.where(jnp.logical_and(u == 2, jnp.logical_not(diag_chip)), qq + 1, qq)
            )
            k = jnp.where(
                kind == 0, j, jnp.where(kind == 1, k_left, jnp.where(kind == 2, k_right, jnp.where(diag_chip, opp, i)))
            )
            work = jnp.where(
                early,
                jnp.logical_or(m < 3, jnp.logical_not(diag_chip)),
                jnp.logical_or(u < 2, jnp.logical_and(u == 2, jnp.logical_or(diag_chip, qq < 2))),
            )

            @pl.when(work)
            def _():
                @pl.when(jnp.logical_and(kind == 3, diag_chip))
                def _():
                    other = pl.ds(pl.multiple_of((1 - c) * rb, rb), rb)
                    wait_recv(sq.at[k, q, :, :, other], d2_recv.at[3, q])

                @pl.when(jnp.logical_not(jnp.logical_and(kind == 3, diag_chip)))
                def _():
                    wait_recv(sq.at[k, q, 1 - c], d2_recv.at[kind, q])

                lhs = jnp.concatenate([rows[buf, k, q, h] for h in range(CORES)], axis=1)
                rhs = sq[k, q].reshape(CORES * qr, cb)
                acc[0:rb] += jnp.dot(lhs, rhs, precision=HIGHEST, preferred_element_type=jnp.float32)

            return carry

        lax.fori_loop(0, PIECES + 3, item2, 0)
        for d in range(2):
            wait_send(sq.at[j, :, c], x2_send.at[d])
        wait_send(sq.at[:, :, c], d2_send.at[0])

        @pl.when(p == 2)
        def _():
            wait_send(sq.at[j, :, c], t_send.at[0])

        t1, t2, t3 = red_get(s + 1)
        mix = (t2 - t3) / (t1 - t2)
        a1 = (1.0 - 2.0 * mix) / (1.0 - mix)
        a2 = (1.0 + mix) / (1.0 - mix)
        a3 = 1.0 / (1.0 - mix)

        def update_body(m, carry):
            at = pl.ds(pl.multiple_of(m * pr, pr), pr)
            x = cols[j, lax.div(m, per), c, piece_rows(m)]
            x2 = sq[j, lax.div(m, per), c, piece_rows(m)]
            new = a1 * x + a2 * x2 - a3 * acc[at]
            put_x(m, new, lax.rem(s + 1, 2))
            return carry + jnp.sum(new * ham_t[at], axis=0, keepdims=True)

        en = lax.fori_loop(0, PIECES, update_body, zero)
        return total_of(en)

    en = lax.fori_loop(0, STEPS, step, jnp.zeros((1, 1), jnp.float32))
    last = STEPS + 1
    red_put(last, [en])
    for q in range(PARTS):
        out[:, q * qr : (q + 1) * qr] = cols[j, q, c].T
    red_send(last)
    red_mid_put(last)
    red_mid_send(last)
    energy[0] = jnp.sum(2.0 * red_get(last)[0])


def solution(mesh):
    def local_fn(ham_blk, bounds, n_occ):
        cb, rb = ham_blk.shape
        qr = rb // PARTS
        f32 = jnp.float32
        dma = pltpu.SemaphoreType.DMA
        vmem = pl.BlockSpec(memory_space=pltpu.VMEM)
        smem = pl.BlockSpec(memory_space=pltpu.SMEM)
        return pl.pallas_call(
            purify,
            out_shape=(jax.ShapeDtypeStruct((cb, rb), f32), jax.ShapeDtypeStruct((1,), f32)),
            in_specs=[vmem, smem, smem],
            out_specs=(vmem, smem),
            scratch_shapes=[
                pltpu.VMEM((RING, PARTS, CORES, qr, cb), f32),
                pltpu.VMEM((2, RING, PARTS, CORES, rb, qr), f32),
                pltpu.VMEM((RING, PARTS, CORES, qr, cb), f32),
                pltpu.VMEM((cb, cb), f32),
                pltpu.VMEM((PARTS, CORES, PARTS, qr, qr), f32),
                pltpu.VMEM((rb, cb), f32),
                pltpu.VMEM((STEPS + 2, RING * CORES, 8, 128), f32),
                pltpu.VMEM((STEPS + 2, RING, 8, 128), f32),
                dma((2, PARTS, 2)), dma((2, PARTS)), dma((2, PARTS, 2)), dma((2, PARTS)), dma((RING, PARTS)),
                dma((2,)), dma((2,)), dma((2,)), dma((2,)), dma((1,)),
                dma((2, PIECES)), dma((4, PARTS)), dma((PARTS, CORES)), dma((2,)), dma((1,)), dma((1,)),
                dma((STEPS + 2,)), dma((STEPS + 2,)), dma((STEPS + 2,)), dma((STEPS + 2,)),
            ],
            compiler_params=pltpu.CompilerParams(
                collective_id=0, has_side_effects=True, vmem_limit_bytes=56 * 2**20
            ),
        )(ham_blk, bounds, n_occ)

    spec_mat = P(("spin", "row"), "col")
    return jax.shard_map(
        local_fn, mesh=mesh, in_specs=(spec_mat, P("spin"), P("spin")), out_specs=(spec_mat, P("spin")), check_vma=False
    )
```

time: 704 us -> 325 us (0.46)
  Pallas kernels: 0 us -> 320 us
  waiting for transfers between devices: 314 us -> 0 us
  blocking collectives: 234 us -> 0 us
  matrix products: 116 us -> 0 us
  between operations: 26 us -> 3.03 us
  other arithmetic: 9.61 us -> 0 us
    pallas_call x0 -> x1, Pallas kernels: none -> 320 us  [local_fn(): pl.pallas_call(purify, out_shape=(jax.ShapeDtypeStruct((cb, rb), f32), ja...]
    all_gather x9 -> x0, waiting for transfers between devices: 312 us -> none  [the longest x3 164 us: local_fn(): x_rows = lax.all_gather(density, 'col', axis=1, tiled=True)]
    psum x5 -> x0, blocking collectives: 234 us -> none  [the longest x3 140 us: local_fn(): traces = lax.psum(part_sums, ('row', 'col'))]
    dot_general x6 -> x0, matrix products: 116 us -> none  [the longest x3 58.4 us: local_fn(): jnp.dot(x_rows, x_cols, precision=highest, preferred_element_type=jnp.flo...]
  transfers between devices with their start and end apart: 9 -> 0, of which waited for: 9 -> 0; matrix products, arithmetic and copies ran while one was open for 1% -> 0% of each run, Pallas kernels for 0% -> 0%
where the time goes in v1:
time: 325 us
  Pallas kernels  320 us (98%)
    pallas_call x1, Pallas kernels, local_fn(): pl.pallas_call(purify, out_shape=(jax.ShapeDtypeStruct((cb, rb), f32), ja...  320 us

profile of v1, /device:TPU:97, one launch (start us, length us, event | category | flops | bytes accessed | tf_op | source)
XLA Modules:
  0.0 325.2 jit_solution(2593803032064097768)
XLA Ops:
  1.3 319.8 %shard_map.50 = (f32[768,384]{1,0:T(8,128)}, f32[1]{0:T(128)}) custom-call(f32[768,384]{1,0:T(8,128)} %ham.1, f32[2]{0:T(128)} %bounds.1, s32[1]{0:T(128)S(6)} %copy.7.n_occ), custom_call_target="tpu_custom_call" | custom-call | tf_op jit(solution)/shard_map/pallas_call | solution.py:384
  321.1 2.4 copy.8

commit v2 on v1

--- a/solution.py
+++ b/solution.py
@@ -223,6 +223,18 @@
             for q in range(PARTS):
                 sq[i, q, c] = acc[rb + q * qr : rb + (q + 1) * qr]
 
+        k_left = jnp.where(p == 1, opp, left)
+        k_right = jnp.where(p == 3, opp, right)
+
+        def send_pieces(lo, hi):
+            @pl.when(jnp.logical_not(diag_chip))
+            def _():
+                for m in range(lo, hi):
+                    for d in range(2):
+                        ref = sq.at[j, m // per, c, pl.ds((m % per) * pr, pr)]
+                        send(ref, x2_send.at[d], x2_recv.at[d, m], to_x[d])
+
+        send_pieces(0, per)
         def sums_body(m, carry):
             x = cols[j, lax.div(m, per), c, piece_rows(m)]
             x2 = acc[pl.ds(pl.multiple_of(m * pr, pr), pr)]
@@ -235,15 +247,8 @@
         sums = lax.fori_loop(0, PIECES, sums_body, (zero, zero, zero))
         red_put(s + 1, [total_of(v) for v in sums])
 
-        k_left = jnp.where(p == 1, opp, left)
-        k_right = jnp.where(p == 3, opp, right)
-
-        @pl.when(jnp.logical_not(diag_chip))
-        def _():
-            for m in range(PIECES):
-                for d in range(2):
-                    ref = sq.at[j, m // per, c, pl.ds((m % per) * pr, pr)]
-                    send(ref, x2_send.at[d], x2_recv.at[d, m], to_x[d])
+        red_send(s + 1)
+        send_pieces(per, PIECES)
 
         @pl.when(p == 2)
         def _():
@@ -260,7 +265,6 @@
             for q in range(PARTS):
                 send(sq.at[i, q, c], d2_send.at[0], d2_recv.at[3, q], partner)
 
-        red_send(s + 1)
         acc[0:rb] = jnp.zeros((rb, cb), jnp.float32)
 
         def arrive2(m):
@@ -295,11 +299,11 @@
             def _():
                 arrive2(m)
 
-            @pl.when(m == 3)
+            @pl.when(m == 6)
             def _():
                 red_mid_put(s + 1)
 
-            @pl.when(m == 4)
+            @pl.when(m == 7)
             def _():
                 red_mid_send(s + 1)
 

time: 325 us -> 284 us (0.87)
  Pallas kernels: 320 us -> 279 us
    pallas_call x1, Pallas kernels: 320 us -> 279 us  [local_fn(): pl.pallas_call(purify, out_shape=(jax.ShapeDtypeStruct((cb, rb), f32), ja...]
where the time goes in v2:
time: 284 us
  Pallas kernels  279 us (98%)
  between operations  3.03 us (1%)
    pallas_call x1, Pallas kernels, local_fn(): pl.pallas_call(purify, out_shape=(jax.ShapeDtypeStruct((cb, rb), f32), ja...  279 us

profile of v2, /device:TPU:97, one launch (start us, length us, event | category | flops | bytes accessed | tf_op | source)
XLA Modules:
  0.0 284.1 jit_solution(11910293561168561978)
XLA Ops:
  1.3 278.7 %shard_map.50 = (f32[768,384]{1,0:T(8,128)}, f32[1]{0:T(128)}) custom-call(f32[768,384]{1,0:T(8,128)} %ham.1, f32[2]{0:T(128)} %bounds.1, s32[1]{0:T(128)S(6)} %copy.7.n_occ), custom_call_target="tpu_custom_call" | custom-call | tf_op jit(solution)/shard_map/pallas_call | solution.py:388
  280.0 2.4 copy.8

commit v3 on v2

--- a/solution.py
+++ b/solution.py
@@ -20,7 +20,7 @@
     ham, bounds, n_occ, out, energy,
     cols, rows, sq, acc, tin, ham_t, red_a, red_b,
     x_recv, xf_recv, y_recv, yf_recv, d_recv, x_send, xf_send, y_send, yf_send, d_send,
-    x2_recv, d2_recv, t_recv, x2_send, d2_send, t_send, a_recv, a_send, b_recv, b_send,
+    x2_recv, d2_recv, t_recv, x2_send, d2_send, t_send, f_send, a_recv, a_send, b_recv, b_send,
 ):
     cb, rb = ham.shape
     qr = rb // PARTS
@@ -225,13 +225,17 @@
 
         k_left = jnp.where(p == 1, opp, left)
         k_right = jnp.where(p == 3, opp, right)
+        d_first = jnp.where(p == 1, 1, 0)
+        k_first = jnp.where(p == 1, k_right, k_left)
+        k_second = jnp.where(p == 1, k_left, k_right)
 
         def send_pieces(lo, hi):
             @pl.when(jnp.logical_not(diag_chip))
             def _():
-                for m in range(lo, hi):
+                for n in range(lo, hi):
                     for d in range(2):
-                        ref = sq.at[j, m // per, c, pl.ds((m % per) * pr, pr)]
+                        m = jnp.where(p == (1 if d == 0 else 3), (n + PIECES - 1) % PIECES, n)
+                        ref = sq.at[j, lax.div(m, per), c, piece_rows(m)]
                         send(ref, x2_send.at[d], x2_recv.at[d, m], to_x[d])
 
         send_pieces(0, per)
@@ -270,18 +274,29 @@
         def arrive2(m):
             q = lax.div(m, per)
             u = lax.rem(m, per)
-            for d, k in ((0, k_left), (1, k_right)):
+
+            @pl.when(jnp.logical_and(p == 2, m == 0))
+            def _():
+                for d, k in ((0, k_left), (1, k_right)):
+                    ref = sq.at[k, PARTS - 1, c, pl.ds((per - 1) * pr, pr)]
+                    wait_recv(ref, x2_recv.at[d, PIECES - 1])
+                    send(ref, f_send.at[d], x2_recv.at[1 - d, PIECES - 1], to_x[d])
+
+            for n, k in enumerate((k_first, k_second)):
+                d = d_first if n == 0 else 1 - d_first
                 ref = sq.at[k, q, c, piece_rows(m)]
-                wait_recv(ref, x2_recv.at[d, m])
-
-                @pl.when(diag_chip)
+
+                @pl.when(jnp.logical_or(p != 2, m < PIECES - 1))
                 def _():
-                    send(ref, x2_send.at[d], x2_recv.at[d, m], to_x[d])
-
-            @pl.when(u == per - 1)
-            def _():
-                send(sq.at[k_left, q, c], d2_send.at[0], d2_recv.at[1, q], partner)
-                send(sq.at[k_right, q, c], d2_send.at[0], d2_recv.at[2, q], partner)
+                    wait_recv(ref, x2_recv.at[d, m])
+
+                @pl.when(jnp.logical_and(diag_chip, m < PIECES - 1))
+                def _():
+                    send(ref, x2_send.at[n], x2_recv.at[n, m], to_x[n])
+
+                @pl.when(u == per - 1)
+                def _():
+                    send(sq.at[k, q, c], d2_send.at[0], d2_recv.at[1 + n, q], partner)
 
             @pl.when(jnp.logical_and(diag_chip, u == per - 2))
             def _():
@@ -315,7 +330,7 @@
                 early, jnp.where(m < 3, m, 0), jnp.where(jnp.logical_and(u == 2, jnp.logical_not(diag_chip)), qq + 1, qq)
             )
             k = jnp.where(
-                kind == 0, j, jnp.where(kind == 1, k_left, jnp.where(kind == 2, k_right, jnp.where(diag_chip, opp, i)))
+                kind == 0, j, jnp.where(kind == 1, k_first, jnp.where(kind == 2, k_second, jnp.where(diag_chip, opp, i)))
             )
             work = jnp.where(
                 early,
@@ -341,13 +356,24 @@
             return carry
 
         lax.fori_loop(0, PIECES + 3, item2, 0)
-        for d in range(2):
-            wait_send(sq.at[j, :, c], x2_send.at[d])
+
+        @pl.when(diag_chip)
+        def _():
+            for d in range(2):
+                wait_send(acc.at[pl.ds(0, (PIECES - 1) * pr)], x2_send.at[d])
+
+        @pl.when(jnp.logical_not(diag_chip))
+        def _():
+            for d in range(2):
+                wait_send(sq.at[j, :, c], x2_send.at[d])
+
         wait_send(sq.at[:, :, c], d2_send.at[0])
 
         @pl.when(p == 2)
         def _():
             wait_send(sq.at[j, :, c], t_send.at[0])
+            for d in range(2):
+                wait_send(sq.at[j, 0, c, pl.ds(0, pr)], f_send.at[d])
 
         t1, t2, t3 = red_get(s + 1)
         mix = (t2 - t3) / (t1 - t2)
@@ -369,9 +395,9 @@
     en = lax.fori_loop(0, STEPS, step, jnp.zeros((1, 1), jnp.float32))
     last = STEPS + 1
     red_put(last, [en])
+    red_send(last)
     for q in range(PARTS):
         out[:, q * qr : (q + 1) * qr] = cols[j, q, c].T
-    red_send(last)
     red_mid_put(last)
     red_mid_send(last)
     energy[0] = jnp.sum(2.0 * red_get(last)[0])
@@ -401,7 +427,7 @@
                 pltpu.VMEM((STEPS + 2, RING, 8, 128), f32),
                 dma((2, PARTS, 2)), dma((2, PARTS)), dma((2, PARTS, 2)), dma((2, PARTS)), dma((RING, PARTS)),
                 dma((2,)), dma((2,)), dma((2,)), dma((2,)), dma((1,)),
-                dma((2, PIECES)), dma((4, PARTS)), dma((PARTS, CORES)), dma((2,)), dma((1,)), dma((1,)),
+                dma((2, PIECES)), dma((4, PARTS)), dma((PARTS, CORES)), dma((2,)), dma((1,)), dma((1,)), dma((2,)),
                 dma((STEPS + 2,)), dma((STEPS + 2,)), dma((STEPS + 2,)), dma((STEPS + 2,)),
             ],
             compiler_params=pltpu.CompilerParams(

time: 284 us -> 281 us (0.989)
  Pallas kernels: 279 us -> 275 us
    pallas_call x1, Pallas kernels: 279 us -> 275 us  [local_fn(): pl.pallas_call(purify, out_shape=(jax.ShapeDtypeStruct((cb, rb), f32), ja...]
where the time goes in v3:
time: 281 us
  Pallas kernels  275 us (98%)
  between operations  3.03 us (1%)
    pallas_call x1, Pallas kernels, local_fn(): pl.pallas_call(purify, out_shape=(jax.ShapeDtypeStruct((cb, rb), f32), ja...  275 us

profile of v3, /device:TPU:97, one launch (start us, length us, event | category | flops | bytes accessed | tf_op | source)
XLA Modules:
  0.0 280.5 jit_solution(6952689622254268859)
XLA Ops:
  1.3 275.1 %shard_map.50 = (f32[768,384]{1,0:T(8,128)}, f32[1]{0:T(128)}) custom-call(f32[768,384]{1,0:T(8,128)} %ham.1, f32[2]{0:T(128)} %bounds.1, s32[1]{0:T(128)S(6)} %copy.7.n_occ), custom_call_target="tpu_custom_call" | custom-call | tf_op jit(solution)/shard_map/pallas_call | solution.py:414
  276.4 2.4 copy.8

commit v4 on v3

--- a/solution.py
+++ b/solution.py
@@ -18,9 +18,9 @@
 
 def purify(
     ham, bounds, n_occ, out, energy,
-    cols, rows, sq, acc, tin, ham_t, red_a, red_b,
+    cols, rows, sq, acc, tin, ham_t, red_a, red_b, red_c,
     x_recv, xf_recv, y_recv, yf_recv, d_recv, x_send, xf_send, y_send, yf_send, d_send,
-    x2_recv, d2_recv, t_recv, x2_send, d2_send, t_send, f_send, a_recv, a_send, b_recv, b_send,
+    x2_recv, d2_recv, t_recv, x2_send, d2_send, t_send, f_send, a_recv, a_send, b_recv, b_send, c_recv, c_send,
 ):
     cb, rb = ham.shape
     qr = rb // PARTS
@@ -105,38 +105,24 @@
                 at = h * rb + q * qr
                 rows[buf, i, q, h, pl.ds(pl.multiple_of(m * pr, pr), pr)] = val[:, at : at + qr]
 
-    barrier = pltpu.get_barrier_semaphore()
-    for k in range(1, n_col):
-        pl.semaphore_signal(barrier, inc=1, device_id={"col": lax.rem(jc + k, n_col)}, device_id_type=MESH)
-    for k in range(1, RING):
-        pl.semaphore_signal(barrier, inc=1, device_id={"row": wrap(i + k)}, device_id_type=MESH)
-    for t in range(cb // qr):
-        ham_t[:, t * qr : (t + 1) * qr] = ham[t * qr : (t + 1) * qr, :].T
-
-    def trace_body(m, tr):
-        blk = ham_t[pl.ds(pl.multiple_of(m * pr, pr), pr)]
-        return tr + jnp.sum(jnp.where(is_diag(m), blk, 0.0), axis=0, keepdims=True)
-
-    tr = lax.fori_loop(0, PIECES, trace_body, jnp.zeros((1, cb), jnp.float32))
-    red_put(0, [total_of(tr)])
-    pl.semaphore_wait(barrier, n_col + RING - 2)
-    red_send(0)
-    red_mid_put(0)
-    red_mid_send(0)
-    mu = red_get(0)[0] / order
-    occ = jnp.full((1, 1), n_occ[0].astype(jnp.float32))
-    eps_min = jnp.full((1, 1), bounds[0])
-    eps_max = jnp.full((1, 1), bounds[1])
-    lam = jnp.minimum(occ / (eps_max - mu), (order - occ) / (mu - eps_min)) / order
-
-    @pl.loop(0, PIECES)
-    def _(m):
-        blk = ham_t[pl.ds(pl.multiple_of(m * pr, pr), pr)]
-        put_x(m, jnp.where(is_diag(m), lam * (mu - blk) + occ / order, -lam * blk), 0)
-
-    def step(s, carry):
-        buf = lax.rem(s, 2)
-
+    others = [
+        {"row": wrap(i + a), "col": lax.rem(jc + b, n_col)} for a in range(RING) for b in range(n_col) if a or b
+    ]
+    me = i * n_col + jc
+
+    def all_put(idx, v):
+        red_c[idx, me] = jnp.zeros((8, 128), jnp.float32) + v
+
+    def all_send(idx):
+        for dev in others:
+            send(red_c.at[idx, me], c_send.at[idx], c_recv.at[idx], dev)
+
+    def all_get(idx):
+        wait_recv(red_c.at[idx, pl.ds(0, len(others))], c_recv.at[idx])
+        wait_send(red_c.at[idx, pl.ds(0, len(others))], c_send.at[idx])
+        return jnp.sum(red_c[idx], axis=0)[0:1, 0:1]
+
+    def send_x(buf):
         for q in range(PARTS):
             for o in range(2):
                 for d in range(2):
@@ -144,6 +130,40 @@
                     send(cols.at[j, q, c, pl.ds(h * hr, hr)], x_send.at[d], x_recv.at[d, q, h], to_x[d])
                     send(rows.at[buf, i, q, h], y_send.at[d], y_recv.at[d, q, h], to_y[d])
             send(cols.at[j, q, c], d_send.at[0], d_recv.at[0, q], partner)
+
+    barrier = pltpu.get_barrier_semaphore()
+    for dev in others:
+        pl.semaphore_signal(barrier, inc=1, device_id=dev, device_id_type=MESH)
+    for t in range(cb // qr):
+        ham_t[:, t * qr : (t + 1) * qr] = ham[t * qr : (t + 1) * qr, :].T
+
+    def trace_body(m, tr):
+        blk = ham_t[pl.ds(pl.multiple_of(m * pr, pr), pr)]
+        return tr + jnp.sum(jnp.where(is_diag(m), blk, 0.0), axis=0, keepdims=True)
+
+    tr = lax.fori_loop(0, PIECES, trace_body, jnp.zeros((1, cb), jnp.float32))
+    all_put(0, total_of(tr))
+
+    @pl.loop(0, PIECES)
+    def _(m):
+        put_x(m, ham_t[pl.ds(pl.multiple_of(m * pr, pr), pr)], 0)
+
+    pl.semaphore_wait(barrier, len(others))
+    all_send(0)
+    send_x(0)
+    mu = all_get(0) / order
+    occ = jnp.full((1, 1), n_occ[0].astype(jnp.float32))
+    eps_min = jnp.full((1, 1), bounds[0])
+    eps_max = jnp.full((1, 1), bounds[1])
+    lam = jnp.minimum(occ / (eps_max - mu), (order - occ) / (mu - eps_min)) / order
+
+    def to_density(v, row0, col0):
+        on = lax.broadcasted_iota(jnp.int32, v.shape, 0) + (row0 - col0) == lax.broadcasted_iota(jnp.int32, v.shape, 1)
+        return jnp.where(on, lam * (mu - v) + occ / order, -lam * v)
+
+    def step(s, carry):
+        buf = lax.rem(s, 2)
+
         acc[...] = jnp.zeros_like(acc)
 
         near = ((left, up), (right, down))
@@ -199,12 +219,27 @@
                 arrive_far(q)
 
             wait_recv(cols.at[k, q, 1 - c], d_recv.at[wrap(k - j), q])
-            rhs = cols[k, q].reshape(CORES * qr, cb)
-            own = cols[k, q, :, :, half_cols].reshape(CORES * qr, rb)
-            lhs = jnp.concatenate(
-                [jnp.concatenate([rows[buf, k, q, h] for h in range(CORES)], axis=1), own.T], axis=0
-            )
-            acc[...] += jnp.dot(lhs, rhs, precision=HIGHEST, preferred_element_type=jnp.float32)
+
+            def product(tile):
+                row0 = k * cb + q * qr
+                rhs = [tile(cols[k, q, h], row0 + h * rb, i * cb) for h in range(CORES)]
+                own = [tile(cols[k, q, h, :, half_cols], row0 + h * rb, i * cb + c * rb) for h in range(CORES)]
+                top = [tile(rows[buf, k, q, h], j * cb + c * rb, row0 + h * rb) for h in range(CORES)]
+                lhs = jnp.concatenate(
+                    [jnp.concatenate(top, axis=1), jnp.concatenate(own, axis=0).T], axis=0
+                )
+                acc[...] += jnp.dot(
+                    lhs, jnp.concatenate(rhs, axis=0), precision=HIGHEST, preferred_element_type=jnp.float32
+                )
+
+            @pl.when(s == 0)
+            def _():
+                product(to_density)
+
+            @pl.when(s > 0)
+            def _():
+                product(lambda v, row0, col0: v)
+
             return carry
 
         lax.fori_loop(0, RING * PARTS, item1, 0)
@@ -239,6 +274,20 @@
                         send(ref, x2_send.at[d], x2_recv.at[d, m], to_x[d])
 
         send_pieces(0, per)
+
+        @pl.when(s == 0)
+        def _():
+            for q in range(PARTS):
+                cols[j, q, c] = to_density(cols[j, q, c], j * cb + c * rb + q * qr, i * cb)
+
+            @pl.loop(0, RING * PARTS)
+            def _(t):
+                k, q = lax.div(t, PARTS), lax.rem(t, PARTS)
+                for h in range(CORES):
+                    rows[buf, k, q, h] = to_density(
+                        rows[buf, k, q, h], j * cb + c * rb, k * cb + h * rb + q * qr
+                    )
+
         def sums_body(m, carry):
             x = cols[j, lax.div(m, per), c, piece_rows(m)]
             x2 = acc[pl.ds(pl.multiple_of(m * pr, pr), pr)]
@@ -298,21 +347,27 @@
                 def _():
                     send(sq.at[k, q, c], d2_send.at[0], d2_recv.at[1 + n, q], partner)
 
-            @pl.when(jnp.logical_and(diag_chip, u == per - 2))
+        def arrive_turned(m):
+            q = lax.div(m, per) - 1
+
+            @pl.when(lax.rem(m, per) == 0)
             def _():
                 for h in range(CORES):
                     wait_recv(tin.at[q, h], t_recv.at[q, h])
                     sq[opp, q, h, :, half_cols] = tin[q, h].reshape(rb, qr).T
 
-            @pl.when(jnp.logical_and(diag_chip, u == per - 1))
-            def _():
-                ref = sq.at[opp, q, :, :, half_cols]
-                send(ref, d2_send.at[0], d2_recv.at[3, q], partner)
+            @pl.when(lax.rem(m, per) == 1)
+            def _():
+                send(sq.at[opp, q, :, :, half_cols], d2_send.at[0], d2_recv.at[3, q], partner)
 
         def item2(m, carry):
             @pl.when(m < PIECES)
             def _():
                 arrive2(m)
+
+            @pl.when(jnp.logical_and(diag_chip, m >= per))
+            def _():
+                arrive_turned(m)
 
             @pl.when(m == 6)
             def _():
@@ -390,17 +445,19 @@
             return carry + jnp.sum(new * ham_t[at], axis=0, keepdims=True)
 
         en = lax.fori_loop(0, PIECES, update_body, zero)
+
+        @pl.when(s < STEPS - 1)
+        def _():
+            send_x(lax.rem(s + 1, 2))
+
         return total_of(en)
 
     en = lax.fori_loop(0, STEPS, step, jnp.zeros((1, 1), jnp.float32))
-    last = STEPS + 1
-    red_put(last, [en])
-    red_send(last)
+    all_put(1, en)
+    all_send(1)
     for q in range(PARTS):
         out[:, q * qr : (q + 1) * qr] = cols[j, q, c].T
-    red_mid_put(last)
-    red_mid_send(last)
-    energy[0] = jnp.sum(2.0 * red_get(last)[0])
+    energy[0] = jnp.sum(2.0 * all_get(1))
 
 
 def solution(mesh):
@@ -425,10 +482,11 @@
                 pltpu.VMEM((rb, cb), f32),
                 pltpu.VMEM((STEPS + 2, RING * CORES, 8, 128), f32),
                 pltpu.VMEM((STEPS + 2, RING, 8, 128), f32),
+                pltpu.VMEM((2, RING * RING * CORES, 8, 128), f32),
                 dma((2, PARTS, 2)), dma((2, PARTS)), dma((2, PARTS, 2)), dma((2, PARTS)), dma((RING, PARTS)),
                 dma((2,)), dma((2,)), dma((2,)), dma((2,)), dma((1,)),
                 dma((2, PIECES)), dma((4, PARTS)), dma((PARTS, CORES)), dma((2,)), dma((1,)), dma((1,)), dma((2,)),
-                dma((STEPS + 2,)), dma((STEPS + 2,)), dma((STEPS + 2,)), dma((STEPS + 2,)),
+                dma((STEPS + 2,)), dma((STEPS + 2,)), dma((STEPS + 2,)), dma((STEPS + 2,)), dma((2,)), dma((2,)),
             ],
             compiler_params=pltpu.CompilerParams(
                 collective_id=0, has_side_effects=True, vmem_limit_bytes=56 * 2**20

time: 281 us -> 270 us (0.961)
  Pallas kernels: 275 us -> 264 us
    pallas_call x1, Pallas kernels: 275 us -> 264 us  [local_fn(): pl.pallas_call(purify, out_shape=(jax.ShapeDtypeStruct((cb, rb), f32), ja...]
where the time goes in v4:
time: 270 us
  Pallas kernels  264 us (98%)
  between operations  3.03 us (1%)
    pallas_call x1, Pallas kernels, local_fn(): pl.pallas_call(purify, out_shape=(jax.ShapeDtypeStruct((cb, rb), f32), ja...  264 us

profile of v4, /device:TPU:97, one launch (start us, length us, event | category | flops | bytes accessed | tf_op | source)
XLA Modules:
  0.0 269.6 jit_solution(6608067888836779820)
XLA Ops:
  1.3 264.2 %shard_map.50 = (f32[768,384]{1,0:T(8,128)}, f32[1]{0:T(128)}) custom-call(f32[768,384]{1,0:T(8,128)} %ham.1, f32[2]{0:T(128)} %bounds.1, s32[1]{0:T(128)S(6)} %copy.7.n_occ), custom_call_target="tpu_custom_call" | custom-call | tf_op jit(solution)/shard_map/pallas_call | solution.py:471
  265.5 2.4 copy.8
